TPU v7x, 8 devices: a whole 2x2x1 slice. The times are simulated.
8 devices in a mesh: part: 1 (over z), model: 2 (over y), data: 4 (over x, core).
Axes of the slice: x: 2, y: 2, z: 1, core: 2. Of those that a mesh axis runs over, the one named last changes fastest.
Arguments:
- hidden: bfloat16 [128, 1, 3840], P(('part', 'data'))
- positions: int32 [128], P(('part', 'data'))
- k_local: bfloat16 [128, 64, 8, 256], P(('part', 'data'), None, 'model')
- v_local: bfloat16 [128, 64, 8, 256], P(('part', 'data'), None, 'model')
- k_global: bfloat16 [128, 256, 8, 256], P(('part', 'data'), None, 'model')
- v_global: bfloat16 [128, 256, 8, 256], P(('part', 'data'), None, 'model')
- w_q: bfloat16 [2, 3840, 16, 256], P(None, 'data', 'model')
- w_k: bfloat16 [2, 3840, 8, 256], P(None, 'data', 'model')
- w_v: bfloat16 [2, 3840, 8, 256], P(None, 'data', 'model')
- w_o: bfloat16 [2, 16, 256, 3840], P(None, 'model', None, 'data')
- w_gate: bfloat16 [2, 3840, 15360], P(None, 'data', 'model')
- w_up: bfloat16 [2, 3840, 15360], P(None, 'data', 'model')
- w_down: bfloat16 [2, 15360, 3840], P(None, 'model', 'data')
- norm_gains: bfloat16 [2, 4, 3840], replicated
Outputs:
- output 1: bfloat16 [128, 1, 3840], P(('part', 'data'))
- output 2: bfloat16 [128, 64, 8, 256], P(('part', 'data'), None, 'model')
- output 3: bfloat16 [128, 64, 8, 256], P(('part', 'data'), None, 'model')
- output 4: bfloat16 [128, 256, 8, 256], P(('part', 'data'), None, 'model')
- output 5: bfloat16 [128, 256, 8, 256], P(('part', 'data'), None, 'model')
All inputs are finite; a program needn't handle non-finite values.
Results may differ from a plain program's by a relative error of at most 0.02.
Values are sent between devices in bfloat16 or wider.
A program may use at most 1 GiB of HBM per device.

v0:
```python
import jax
import jax.numpy as jnp
from jax import lax
from jax.sharding import PartitionSpec as P

SOFT_CAP = 50.0
NORM_EPS = 1e-6
ROPE_BASE = 10000.0

ROW_SPEC = P(("part", "data"), None, None)
POS_SPEC = P(("part", "data"))
CACHE_SPEC = P(("part", "data"), None, "model", None)
PROJ_IN_SPEC = P(None, "data", "model", None)
PROJ_OUT_SPEC = P(None, "model", None, "data")
FF_IN_SPEC = P(None, "data", "model")
FF_OUT_SPEC = P(None, "model", "data")
GAIN_SPEC = P(None, None, None)


def rms_norm(hidden, gain):
    mean_sq = jnp.mean(jnp.square(hidden), axis=-1, keepdims=True)
    return hidden * lax.rsqrt(mean_sq + NORM_EPS) * (1.0 + gain.astype(jnp.float32))


def rotary(hidden, cos_t, sin_t):
    half_dim = hidden.shape[-1] // 2
    first_half = hidden[..., :half_dim]
    second_half = hidden[..., half_dim:]
    return jnp.concatenate([first_half * cos_t - second_half * sin_t, second_half * cos_t + first_half * sin_t], axis=-1)


def rope_tables(positions, head_dim):
    inv_freq = ROPE_BASE ** (-jnp.arange(0, head_dim, 2).astype(jnp.float32) / head_dim)
    angles = positions.astype(jnp.float32)[:, None] * inv_freq[None, :]
    return jnp.cos(angles)[:, None, :], jnp.sin(angles)[:, None, :]


def attend(q_new, k_new, v_new, positions, k_cache, v_cache, is_local):
    n_rows, cache_len, kv_loc, head_dim = k_cache.shape
    group_size = q_new.shape[1] // kv_loc
    slot_ids = jnp.arange(cache_len)
    if is_local:
        slot_now = positions % cache_len
        valid_mask = ((positions[:, None] - slot_ids[None, :]) % cache_len) <= positions[:, None]
    else:
        slot_now = positions
        valid_mask = slot_ids[None, :] <= positions[:, None]
    slot_hit = (slot_ids[None, :] == slot_now[:, None])[:, :, None, None]
    k_cache = jnp.where(slot_hit, k_new[:, None], k_cache)
    v_cache = jnp.where(slot_hit, v_new[:, None], v_cache)
    q_grp = q_new.reshape(n_rows, kv_loc, group_size, head_dim)
    scores = jnp.einsum("bkgd,btkd->bkgt", q_grp, k_cache, preferred_element_type=jnp.float32)
    scores = SOFT_CAP * jnp.tanh(scores / SOFT_CAP)
    scores = jnp.where(valid_mask[:, None, None, :], scores, -1e30)
    attn_prob = jax.nn.softmax(scores, axis=-1).astype(jnp.bfloat16)
    head_out = jnp.einsum("bkgt,btkd->bkgd", attn_prob, v_cache, preferred_element_type=jnp.float32)
    return head_out.astype(jnp.bfloat16).reshape(n_rows, kv_loc * group_size, head_dim), k_cache, v_cache


def layer_block(hidden, positions, k_cache, v_cache, weights, layer, is_local):
    w_q, w_k, w_v, w_o, w_gate, w_up, w_down, norm_gains = weights
    layer_gains = norm_gains[layer]
    wq_full = lax.all_gather(w_q[layer], "data", axis=0, tiled=True)
    wk_full = lax.all_gather(w_k[layer], "data", axis=0, tiled=True)
    wv_full = lax.all_gather(w_v[layer], "data", axis=0, tiled=True)
    wo_full = lax.all_gather(w_o[layer], "data", axis=2, tiled=True)
    wg_full = lax.all_gather(w_gate[layer], "data", axis=0, tiled=True)
    wu_full = lax.all_gather(w_up[layer], "data", axis=0, tiled=True)
    wd_full = lax.all_gather(w_down[layer], "data", axis=1, tiled=True)
    residual = hidden[:, 0, :].astype(jnp.float32)
    normed = rms_norm(residual, layer_gains[0]).astype(jnp.bfloat16)
    q_proj = jnp.einsum("bd,dhk->bhk", normed, wq_full, preferred_element_type=jnp.float32)
    k_proj = jnp.einsum("bd,dhk->bhk", normed, wk_full, preferred_element_type=jnp.float32)
    v_proj = jnp.einsum("bd,dhk->bhk", normed, wv_full, preferred_element_type=jnp.float32)
    head_dim = q_proj.shape[-1]
    cos_t, sin_t = rope_tables(positions, head_dim)
    q_new = (rotary(q_proj, cos_t, sin_t) * head_dim ** -0.5).astype(jnp.bfloat16)
    k_new = rotary(k_proj, cos_t, sin_t).astype(jnp.bfloat16)
    head_out, k_cache, v_cache = attend(q_new, k_new, v_proj.astype(jnp.bfloat16), positions, k_cache, v_cache, is_local)
    attn_sum = lax.psum(jnp.einsum("bhk,hkd->bd", head_out, wo_full, preferred_element_type=jnp.float32), "model")
    mid_hidden = (residual + rms_norm(attn_sum, layer_gains[1])).astype(jnp.bfloat16)
    mid_f = mid_hidden.astype(jnp.float32)
    normed_ff = rms_norm(mid_f, layer_gains[2]).astype(jnp.bfloat16)
    gate_proj = jnp.dot(normed_ff, wg_full, preferred_element_type=jnp.float32)
    up_proj = jnp.dot(normed_ff, wu_full, preferred_element_type=jnp.float32)
    gated_act = (jax.nn.gelu(gate_proj, approximate=True) * up_proj).astype(jnp.bfloat16)
    down_sum = lax.psum(jnp.dot(gated_act, wd_full, preferred_element_type=jnp.float32), "model")
    layer_out = (mid_f + rms_norm(down_sum, layer_gains[3])).astype(jnp.bfloat16)
    return layer_out[:, None, :], k_cache, v_cache


def solution(mesh):
    def device_step(hidden, positions, k_local, v_local, k_global, v_global, w_q, w_k, w_v, w_o, w_gate, w_up, w_down, norm_gains):
        weights = (w_q, w_k, w_v, w_o, w_gate, w_up, w_down, norm_gains)
        mid_hidden, k_local, v_local = layer_block(hidden, positions, k_local, v_local, weights, 0, True)
        final, k_global, v_global = layer_block(mid_hidden, positions, k_global, v_global, weights, 1, False)
        return final, k_local, v_local, k_global, v_global

    in_specs = (ROW_SPEC, POS_SPEC, CACHE_SPEC, CACHE_SPEC, CACHE_SPEC, CACHE_SPEC, PROJ_IN_SPEC, PROJ_IN_SPEC, PROJ_IN_SPEC, PROJ_OUT_SPEC, FF_IN_SPEC, FF_IN_SPEC, FF_OUT_SPEC, GAIN_SPEC)
    out_specs = (ROW_SPEC, CACHE_SPEC, CACHE_SPEC, CACHE_SPEC, CACHE_SPEC)
    return jax.shard_map(device_step, mesh=mesh, in_specs=in_specs, out_specs=out_specs, check_vma=False)
```

profile of v0, /device:TPU:0, one launch (start us, length us, event | category | flops | bytes accessed | tf_op | source)
XLA Modules:
  0.0 2937.5 jit_solution(744112525591659900)
XLA Ops:
  7.2 3.9 fusion.175
  11.1 1.5 copy.68
  12.7 3.8 fusion.176
  16.5 1.5 copy.69
  18.1 4.9 fusion.174
  23.0 2.7 copy.67
  25.8 4.9 fusion.173
  30.7 4.2 copy.70
  35.5 0.9 add_reduce_fusion
  36.8 31.5 %all-gather.31.cloned.1.call-done = bf16[1,3840,4,256]{3,1,2,0:T(8,128)(2,1)} async-done(((bf16[1,960,4,256]{3,1,2,0:T(8,128)(2,1)}), bf16[1,3840,4,256]{3,1,2,0:T(8,128)(2,1)}) %all-gather.31.cloned.1.call-update) | async-done | bytes 7864336 | tf_op jit(solution)/shard_map/all_gather | solution.py:64
  68.3 4.7 fusion.44
  73.2 50.0 %all-gather.33.cloned.1.call-done = bf16[1,3840,4,256]{3,1,2,0:T(8,128)(2,1)} async-done(((bf16[1,960,4,256]{3,1,2,0:T(8,128)(2,1)}), bf16[1,3840,4,256]{3,1,2,0:T(8,128)(2,1)}) %all-gather.33.cloned.1.call-update) | async-done | bytes 7864336 | tf_op jit(solution)/shard_map/all_gather | solution.py:65
  123.2 4.7 fusion.81
  128.0 8.5 broadcast_select_fusion.3
  136.4 87.0 %all-gather.29.cloned.1.call-done = bf16[1,3840,8,256]{3,1,2,0:T(8,128)(2,1)} async-done(((bf16[1,960,8,256]{3,1,2,0:T(8,128)(2,1)}), bf16[1,3840,8,256]{3,1,2,0:T(8,128)(2,1)}) %all-gather.29.cloned.1.call-update) | async-done | bytes 15728656 | tf_op jit(solution)/shard_map/all_gather | solution.py:63
  223.4 8.3 fusion.24
  232.0 3.6 fusion.178
  235.6 2.9 fusion.59
  238.6 85.0 %all-gather.35.cloned.1.call-done = bf16[1,8,256,3840]{2,1,0,3:T(8,128)(2,1)} async-done(((bf16[1,8,256,960]{2,1,0,3:T(8,128)(2,1)}), bf16[1,8,256,3840]{2,1,0,3:T(8,128)(2,1)}) %all-gather.35.cloned.1.call-update) | async-done | bytes 15728656 | tf_op jit(solution)/shard_map/all_gather | solution.py:66
  323.6 20.3 copy.51
  343.8 9.1 fusion.46
  352.9 20.6 fusion.171
  373.6 20.5 fusion.170
  394.3 20.6 fusion.172
  414.9 10.4 all-gather.49.cloned.1.call-start
  425.3 6.3 copy.74
  431.7 1.2 multiply_reduce_fusion.3
  432.9 1.3 fusion.118
  434.2 287.6 %all-gather.37.cloned.1.call-done = bf16[1,3840,7680]{2,1,0:T(8,128)(2,1)} async-done(((bf16[1,960,7680]{2,1,0:T(8,128)(2,1)}), bf16[1,3840,7680]{2,1,0:T(8,128)(2,1)}) %all-gather.37.cloned.1.call-update) | async-done | bytes 58982416 | tf_op jit(solution)/shard_map/all_gather | solution.py:67
  721.8 21.6 fusion.106
  743.4 324.6 %all-gather.39.cloned.1.call-done = bf16[1,3840,7680]{2,1,0:T(8,128)(2,1)} async-done(((bf16[1,960,7680]{2,1,0:T(8,128)(2,1)}), bf16[1,3840,7680]{2,1,0:T(8,128)(2,1)}) %all-gather.39.cloned.1.call-update) | async-done | bytes 58982416 | tf_op jit(solution)/shard_map/all_gather | solution.py:68
  1068.0 346.8 %all-gather.41.cloned.1.call-done = bf16[1,7680,3840]{1,2,0:T(8,128)(2,1)} async-done(((bf16[1,7680,960]{1,2,0:T(8,128)(2,1)}), bf16[1,7680,3840]{1,2,0:T(8,128)(2,1)}) %all-gather.41.cloned.1.call-update) | async-done | bytes 58982416 | tf_op jit(solution)/shard_map/all_gather | solution.py:69
  1414.8 41.3 %fusion.8 = f32[32,3840]{1,0:T(8,128)} fusion(bf16[1,7680,3840]{1,2,0:T(8,128)(2,1)} %all-gather.41.cloned.1.call-done, f32[32,7680]{1,0:T(8,128)S(1)} %fusion.106, bf16[1,3840,7680]{2,1,0:T(8,128)(2,1)} %all-gather.39.cloned.1.call-done, bf16[32,3840]{1,0:T(8,128)(2,1)S(1)} %get-tuple-element.18, f32[3840]{0:T(1024)S(1)} %get-tuple-element.9, ...), kind=kOutput, calls=%fused_computation.8 | convolution fusion | flops 3775856640 | bytes 119700608 | tf_op jit(solution)/shard_map/dot_general | solution.py:87
  1456.2 5.0 copy.71
  1461.2 3.1 copy.73
  1464.4 1.5 copy.72
  1466.1 48.4 %all-gather.49.cloned.1.call-done = bf16[1,8,256,3840]{2,1,0,3:T(8,128)(2,1)} async-done(((bf16[1,8,256,960]{2,1,0,3:T(8,128)(2,1)}), bf16[1,8,256,3840]{2,1,0,3:T(8,128)(2,1)}) %all-gather.49.cloned.1.call-update) | async-done | bytes 15728656 | tf_op jit(solution)/shard_map/all_gather | solution.py:66
  1514.5 20.4 copy.63
  1534.8 3.9 all-reduce.7.cloned.1.call-done
  1538.8 1.2 multiply_reduce_fusion.2
  1540.0 1.3 fusion.122
  1541.3 97.8 %all-gather.43.cloned.1.call-done = bf16[1,3840,8,256]{3,1,2,0:T(8,128)(2,1)} async-done(((bf16[1,960,8,256]{3,1,2,0:T(8,128)(2,1)}), bf16[1,3840,8,256]{3,1,2,0:T(8,128)(2,1)}) %all-gather.43.cloned.1.call-update) | async-done | bytes 15728656 | tf_op jit(solution)/shard_map/all_gather | solution.py:63
  1639.0 8.3 fusion.20
  1647.6 45.5 %all-gather.47.cloned.1.call-done = bf16[1,3840,4,256]{3,1,2,0:T(8,128)(2,1)} async-done(((bf16[1,960,4,256]{3,1,2,0:T(8,128)(2,1)}), bf16[1,3840,4,256]{3,1,2,0:T(8,128)(2,1)}) %all-gather.47.cloned.1.call-update) | async-done | bytes 7864336 | tf_op jit(solution)/shard_map/all_gather | solution.py:65
  1693.2 4.7 fusion.84
  1698.0 50.0 %all-gather.45.cloned.1.call-done = bf16[1,3840,4,256]{3,1,2,0:T(8,128)(2,1)} async-done(((bf16[1,960,4,256]{3,1,2,0:T(8,128)(2,1)}), bf16[1,3840,4,256]{3,1,2,0:T(8,128)(2,1)}) %all-gather.45.cloned.1.call-update) | async-done | bytes 7864336 | tf_op jit(solution)/shard_map/all_gather | solution.py:64
  1748.0 4.7 fusion.40
  1752.8 23.0 broadcast_select_fusion.1
  1775.8 10.4 fusion.179
  1786.2 8.1 fusion.62
  1794.3 9.1 fusion.49
  1803.5 0.5 all-gather.51.cloned.1.call-update
  1804.6 0.5 all-gather.55.cloned.1.call-update
  1805.2 20.5 all-reduce.9.cloned.1.call-done
  1825.7 1.2 multiply_reduce_fusion.1
  1826.9 1.3 fusion.126
  1828.2 343.5 %all-gather.51.cloned.1.call-done = bf16[1,3840,7680]{2,1,0:T(8,128)(2,1)} async-done(((bf16[1,960,7680]{2,1,0:T(8,128)(2,1)}), bf16[1,3840,7680]{2,1,0:T(8,128)(2,1)}) %all-gather.51.cloned.1.call-update) | async-done | bytes 58982416 | tf_op jit(solution)/shard_map/all_gather | solution.py:67
  2171.8 21.8 fusion.115
  2193.6 324.2 %all-gather.53.cloned.1.call-done = bf16[1,3840,7680]{2,1,0:T(8,128)(2,1)} async-done(((bf16[1,960,7680]{2,1,0:T(8,128)(2,1)}), bf16[1,3840,7680]{2,1,0:T(8,128)(2,1)}) %all-gather.53.cloned.1.call-update) | async-done | bytes 58982416 | tf_op jit(solution)/shard_map/all_gather | solution.py:68
  2517.8 346.0 %all-gather.55.cloned.1.call-done = bf16[1,7680,3840]{1,2,0:T(8,128)(2,1)} async-done(((bf16[1,7680,960]{1,2,0:T(8,128)(2,1)}), bf16[1,7680,3840]{1,2,0:T(8,128)(2,1)}) %all-gather.55.cloned.1.call-update) | async-done | bytes 58982416 | tf_op jit(solution)/shard_map/all_gather | solution.py:69
  2863.9 41.2 %fusion.2 = f32[32,3840]{1,0:T(8,128)} fusion(bf16[1,7680,3840]{1,2,0:T(8,128)(2,1)} %all-gather.55.cloned.1.call-done, f32[32,7680]{1,0:T(8,128)S(1)} %fusion.115, bf16[1,3840,7680]{2,1,0:T(8,128)(2,1)} %all-gather.53.cloned.1.call-done, bf16[32,3840]{1,0:T(8,128)(2,1)S(1)} %get-tuple-element.14, f32[3840]{0:T(1024)S(1)} %copy-done.2, ...), kind=kOutput, calls=%fused_computation.2 | convolution fusion | flops 3775856640 | bytes 119700608 | tf_op jit(solution)/shard_map/dot_general | solution.py:87
  2905.1 22.3 all-reduce.11.cloned.1.call-done
  2927.3 1.2 multiply_reduce_fusion
  2928.5 1.9 fusion.137
  (93 shorter events, 3.4 us)
Async XLA Ops:
  7.2 61.2 %all-gather.31.cloned.1.call-start = ((), (), s32[]{:S(2)}) async-start(), calls=%async_computation.5 | async-start | bytes 9830400 | tf_op jit(solution)/shard_map/all_gather | solution.py:64
  12.6 110.5 %all-gather.33.cloned.1.call-start = ((), (), s32[]{:S(2)}) async-start(), calls=%async_computation.6 | async-start | bytes 9830400 | tf_op jit(solution)/shard_map/all_gather | solution.py:65
  18.1 205.4 %all-gather.29.cloned.1.call-start = ((), (), s32[]{:S(2)}) async-start(), calls=%async_computation.4 | async-start | bytes 19660800 | tf_op jit(solution)/shard_map/all_gather | solution.py:63
  25.7 9.7 copy-start.1
  25.7 9.8 copy-start.8
  25.7 10.8 copy-start.12
  25.7 297.8 %all-gather.35.cloned.1.call-start = ((), (), s32[]{:S(2)}) async-start(), calls=%async_computation.7 | async-start | bytes 19660800 | tf_op jit(solution)/shard_map/all_gather | solution.py:66
  34.9 396.7 %all-reduce.5.cloned.1.call-start = ((), (), s32[]{:S(2)}) async-start(), calls=%async_computation | async-start | bytes 983040 | tf_op jit(solution)/shard_map/psum | solution.py:80
  36.8 194.9 %copy-start.3 = (f32[32,128]{1,0:T(8,128)}, f32[32,128]{1,0:T(8,128)S(1)}, u32[]{:S(2)}) copy-start(f32[32,128]{1,0:T(8,128)S(1)} %get-tuple-element.45) | copy-start | bytes 49156
  36.8 194.9 %copy-start.5 = (f32[32,128]{1,0:T(8,128)}, f32[32,128]{1,0:T(8,128)S(1)}, u32[]{:S(2)}) copy-start(f32[32,128]{1,0:T(8,128)S(1)} %get-tuple-element.46) | copy-start | bytes 49156
  352.9 368.9 %all-gather.37.cloned.1.call-start = ((), (), s32[]{:S(2)}) async-start(), calls=%async_computation.8 | async-start | bytes 73728000 | tf_op jit(solution)/shard_map/all_gather | solution.py:67
  373.6 694.4 %all-gather.39.cloned.1.call-start = ((), (), s32[]{:S(2)}) async-start(), calls=%async_computation.9 | async-start | bytes 73728000 | tf_op jit(solution)/shard_map/all_gather | solution.py:68
  394.2 1020.6 %all-gather.41.cloned.1.call-start = ((), (), s32[]{:S(2)}) async-start(), calls=%async_computation.10 | async-start | bytes 73728000 | tf_op jit(solution)/shard_map/all_gather | solution.py:69
  414.9 1099.5 %all-gather.49.cloned.1.call-start = ((), (), s32[]{:S(2)}) async-start(), calls=%async_computation.14 | async-start | bytes 19660800 | tf_op jit(solution)/shard_map/all_gather | solution.py:66
  431.6 1107.2 %all-reduce.7.cloned.1.call-start = ((), (), s32[]{:S(2)}) async-start(), calls=%async_computation.1 | async-start | bytes 983040 | tf_op jit(solution)/shard_map/psum | solution.py:87
  1456.1 8.3 copy-start
  1456.1 9.9 copy-start.13
  1456.1 182.9 %all-gather.43.cloned.1.call-start = ((), (), s32[]{:S(2)}) async-start(), calls=%async_computation.11 | async-start | bytes 19660800 | tf_op jit(solution)/shard_map/all_gather | solution.py:63
  1461.2 232.0 %all-gather.47.cloned.1.call-start = ((), (), s32[]{:S(2)}) async-start(), calls=%async_computation.13 | async-start | bytes 9830400 | tf_op jit(solution)/shard_map/all_gather | solution.py:65
  1464.3 283.7 %all-gather.45.cloned.1.call-start = ((), (), s32[]{:S(2)}) async-start(), calls=%async_computation.12 | async-start | bytes 9830400 | tf_op jit(solution)/shard_map/all_gather | solution.py:64
  1465.9 359.8 %all-reduce.9.cloned.1.call-start = ((), (), s32[]{:S(2)}) async-start(), calls=%async_computation.2 | async-start | bytes 983040 | tf_op jit(solution)/shard_map/psum | solution.py:80
  1466.1 73.9 %copy-start.11 = (f32[3840]{0:T(1024)S(1)}, f32[3840]{0:T(1024)}, u32[]{:S(2)}) copy-start(f32[3840]{0:T(1024)} %get-tuple-element.8) | copy-start | bytes 46084
  1466.1 173.0 %copy-start.7 = (f32[3840]{0:T(1024)S(1)}, f32[3840]{0:T(1024)}, u32[]{:S(2)}) copy-start(f32[3840]{0:T(1024)} %get-tuple-element.7) | copy-start | bytes 46084
  1534.8 112.5 %copy-start.4 = (f32[32,128]{1,0:T(8,128)S(1)}, f32[32,128]{1,0:T(8,128)}, u32[]{:S(2)}) copy-start(f32[32,128]{1,0:T(8,128)} %copy-done.3) | copy-start | bytes 49156
  1534.8 112.5 %copy-start.6 = (f32[32,128]{1,0:T(8,128)S(1)}, f32[32,128]{1,0:T(8,128)}, u32[]{:S(2)}) copy-start(f32[32,128]{1,0:T(8,128)} %copy-done.5) | copy-start | bytes 49156
  1803.4 368.3 %all-gather.51.cloned.1.call-start = ((), (), s32[]{:S(2)}) async-start(), calls=%async_computation.15 | async-start | bytes 73728000 | tf_op jit(solution)/shard_map/all_gather | solution.py:67
  1804.0 713.8 %all-gather.53.cloned.1.call-start = ((), (), s32[]{:S(2)}) async-start(), calls=%async_computation.16 | async-start | bytes 73728000 | tf_op jit(solution)/shard_map/all_gather | solution.py:68
  1804.1 22.8 copy-start.10
  1804.1 367.7 %copy-start.2 = (f32[3840]{0:T(1024)S(1)}, f32[3840]{0:T(1024)}, u32[]{:S(2)}) copy-start(f32[3840]{0:T(1024)} %get-tuple-element.12) | copy-start | bytes 46084
  1804.6 1059.3 %all-gather.55.cloned.1.call-start = ((), (), s32[]{:S(2)}) async-start(), calls=%async_computation.17 | async-start | bytes 73728000 | tf_op jit(solution)/shard_map/all_gather | solution.py:69
  1805.2 1122.2 %all-reduce.11.cloned.1.call-start = ((), (), s32[]{:S(2)}) async-start(), calls=%async_computation.3 | async-start | bytes 983040 | tf_op jit(solution)/shard_map/psum | solution.py:87
  2193.6 734.9 %copy-start.9 = (f32[3840]{0:T(1024)S(1)}, f32[3840]{0:T(1024)}, u32[]{:S(2)}) copy-start(f32[3840]{0:T(1024)} %get-tuple-element.5) | copy-start | bytes 46084
Sparse Core Ops, SparseCore 0:
  12.8 55.5 all-gather.30
  70.4 52.6 all-gather.32
  125.3 98.1 all-gather.28
  225.4 98.1 all-gather.34
  353.0 22.1 all-reduce.4
  377.1 344.6 all-gather.36
  723.3 344.6 all-gather.38
  1070.1 344.6 all-gather.40
  1416.3 98.1 all-gather.48
  1516.6 22.1 all-reduce.6
  1540.9 98.1 all-gather.42
  1640.4 52.6 all-gather.46
  1695.3 52.6 all-gather.44
  1803.5 22.1 all-reduce.8
  1827.1 344.6 all-gather.50
  2173.2 344.6 all-gather.52
  2519.2 344.6 all-gather.54
  2905.2 22.1 all-reduce.10
where the time goes:
time: 2940 us
  waiting for transfers between devices  2520 us (86%)
  matrix products  205 us (7%)
  local copies, waits for them, and re-layouts  146 us (5%)
  other arithmetic  43.6 us (1%)
    all_gather x2, waiting for transfers between devices, layer_block(): wd_full = lax.all_gather(w_down[layer], 'data', axis=1, tiled=True)  693 us
    all_gather x2, waiting for transfers between devices, layer_block(): wu_full = lax.all_gather(w_up[layer], 'data', axis=0, tiled=True)  649 us
    all_gather x2, waiting for transfers between devices, layer_block(): wg_full = lax.all_gather(w_gate[layer], 'data', axis=0, tiled=True)  631 us
    all_gather x2, waiting for transfers between devices, layer_block(): wq_full = lax.all_gather(w_q[layer], 'data', axis=0, tiled=True)  185 us
    all_gather x2, waiting for transfers between devices, layer_block(): wo_full = lax.all_gather(w_o[layer], 'data', axis=2, tiled=True)  133 us
    all_gather x2, waiting for transfers between devices, layer_block(): wv_full = lax.all_gather(w_v[layer], 'data', axis=0, tiled=True)  95.5 us
    dot_general x2, matrix products, layer_block(): jnp.dot(gated_act, wd_full, preferred_element_type=jnp.float32)  82.5 us
    all_gather x2, waiting for transfers between devices, layer_block(): wk_full = lax.all_gather(w_k[layer], 'data', axis=0, tiled=True)  81.5 us
  transfers between devices with their start and end apart: 18, of which 17 were waited for; matrix products, arithmetic and copies ran while one was open for 9% of the time, Pallas kernels for 0%

commit v1 on v0

v1 whole, which is shorter than its diff:
```python
import functools

import jax
import jax.numpy as jnp
from jax import lax
from jax.experimental import pallas as pl
from jax.experimental.pallas import tpu as pltpu
from jax.sharding import PartitionSpec as P

SOFT_CAP = 50.0
NORM_EPS = 1e-6
ROPE_BASE = 10000.0

ROW_SPEC = P(("part", "data"), None, None)
POS_SPEC = P(("part", "data"))
CACHE_SPEC = P(("part", "data"), None, "model", None)
PROJ_IN_SPEC = P(None, "data", "model", None)
PROJ_OUT_SPEC = P(None, "model", None, "data")
FF_IN_SPEC = P(None, "data", "model")
FF_OUT_SPEC = P(None, "model", "data")
GAIN_SPEC = P(None, None, None)

MESH = pl.DeviceIdType.MESH
F32, BF16 = jnp.float32, jnp.bfloat16

ROWS = 32
OWN = 16
ALL = 128
WID = 960
FF = 7680
CH = 768
NC = FF // CH
WSLOTS = 3
QW = 4096
QCH = 1024
NQ = QW // QCH
OCH = 1024
NO = 2
NT = (((1,), (1,)), ((), ()))


class Place:
    def __init__(self):
        self.m = lax.axis_index("model")
        self.d = lax.axis_index("data")
        self.x = self.d // 2
        self.c = self.d % 2
        self.me = self.m * 4 + self.d
        self.block = self.c * 2 + self.x
        self.xblock = self.c * 2 + (1 - self.x)
        self.xpeer = {"model": self.m, "data": (1 - self.x) * 2 + self.c}
        self.partner = {"model": self.m, "data": self.x * 2 + (1 - self.c)}

    def other(self, o):
        om, ox, oc = o // 4, (o // 2) % 2, o % 2
        flip = lambda v, b: (1 - v) if b else v
        m, x, c = flip(self.m, om), flip(self.x, ox), flip(self.c, oc)
        return m, x, c, {"model": m, "data": x * 2 + c}


def rcopy(src, dst, ssem, rsem, dev):
    return pltpu.make_async_remote_copy(src_ref=src, dst_ref=dst, send_sem=ssem, recv_sem=rsem, device_id=dev, device_id_type=MESH)


def rows_at(start, size):
    return pl.ds(pl.multiple_of(start, size), size)


def barrier_all(pc):
    sem = pltpu.get_barrier_semaphore()
    for o in range(1, 8):
        pl.semaphore_signal(sem, inc=1, device_id=pc.other(o)[3], device_id_type=MESH)
    pl.semaphore_wait(sem, 7)


def spread_rows(pc, parts, hsend, hall, ssem, rsem):
    for i in range(4):
        hsend[i] = parts[i]
    mine = rows_at(pc.block * ROWS + pc.m * OWN, OWN)
    copies = []
    for o in range(1, 8):
        m, x, c, dev = pc.other(o)
        cp = rcopy(hsend.at[x * 2 + c], hall.at[mine, :], ssem.at[o], rsem.at[o], dev)
        cp.start()
        copies.append(cp)
    hall[mine, :] = hsend[pc.d]
    for cp in copies:
        cp.wait()


def scatter_sums(pc, acc, r3, ssem, rsem):
    copies = []
    for o in range(1, 8):
        m, x, c, dev = pc.other(o)
        src = rows_at((c * 2 + x) * ROWS + m * OWN, OWN)
        cp = rcopy(acc.at[src, :], r3.at[pc.me], ssem.at[o], rsem.at[o], dev)
        cp.start()
        copies.append(cp)
    r3[pc.me] = acc[rows_at(pc.block * ROWS + pc.m * OWN, OWN), :]
    for cp in copies:
        cp.wait()


def norm_parts(parts, gains):
    total = sum(jnp.sum(p * p, axis=-1, keepdims=True) for p in parts)
    inv = lax.rsqrt(total / (4 * WID) + NORM_EPS)
    return [p * inv * (1.0 + gains[i]) for i, p in enumerate(parts)]


def gain_rows(gains, layer, k):
    g = gains[layer, k].astype(F32)
    return [g[i:i + 1] for i in range(4)]


def after_sum(res, r3, gain):
    sums = [r3[i] + r3[4 + i] for i in range(4)]
    normed = norm_parts(sums, gain)
    return [(res[i].astype(F32) + normed[i]).astype(BF16) for i in range(4)]


def next_norm(mids, gain):
    return [p.astype(BF16) for p in norm_parts([p.astype(F32) for p in mids], gain)]


def loop(n, body):
    lax.fori_loop(0, n, lambda t, z: (body(t), z)[1], 0)


def project(pc, s, hall, w_hbm_at, out):
    keep, away = pc.c * 64, (1 - pc.c) * 64
    d2d = lambda t: rcopy(s["qp"].at[t, rows_at(away, 64), :], s["qr1"].at[t], s["q_s"].at[0, t], s["q_r"].at[0, t], pc.partner)
    xco = lambda t: rcopy(s["qs1"].at[t], s["qr2"].at[t], s["q_s"].at[1, t], s["q_r"].at[1, t], pc.xpeer)

    def second(k):
        d2d(k).wait_recv()
        o = 1 - pc.x
        s["qs1"][k] = s["qp"][k, rows_at(keep + o * ROWS, ROWS), :] + s["qr1"][k, rows_at(o * ROWS, ROWS), :]
        xco(k).start()

    for t in range(NQ):
        pltpu.make_async_copy(w_hbm_at(t), s["wq"].at[t], s["wq_sem"].at[t]).wait()
        s["qp"][t] = jnp.dot(hall[...], s["wq"][t], preferred_element_type=F32)
        d2d(t).start()
        if t:
            second(t - 1)
    second(NQ - 1)
    for t in range(NQ):
        xco(t).wait_recv()
        own = s["qp"][t, rows_at(keep + pc.x * ROWS, ROWS), :] + s["qr1"][t, rows_at(pc.x * ROWS, ROWS), :]
        out[:, t * QCH:(t + 1) * QCH] = own + s["qr2"][t]
    for t in range(NQ):
        d2d(t).wait_send()
        xco(t).wait_send()


def start_project_weights(s, w_hbm_at):
    for t in range(NQ):
        pltpu.make_async_copy(w_hbm_at(t), s["wq"].at[t], s["wq_sem"].at[t]).start()


def feed_forward(pc, s, layer, hall, wg, wu, wd, acc):
    keep, away = pc.c * 64, (1 - pc.c) * 64

    def cols(t):
        return pl.ds(pl.multiple_of(t * CH, CH), CH)

    def w_copy(i, t):
        ref = (wg, wu)[i]
        return pltpu.make_async_copy(ref.at[layer, :, cols(t)], s["w"].at[t % WSLOTS, i], s["w_sem"].at[t % WSLOTS, i])

    def wd_copy(t):
        return pltpu.make_async_copy(wd.at[layer, :, cols(t)], s["wd"].at[t], s["wd_sem"].at[t])

    def sems(i, t):
        return s["f_s"].at[i, t], s["f_r"].at[i, t]

    d2d = lambda t: rcopy(s["p"].at[t, :, rows_at(away, 64), :], s["r1"].at[t], *sems(0, t), pc.partner)
    xco = lambda t: rcopy(s["s1"].at[t], s["r2"].at[t], *sems(1, t), pc.xpeer)
    mine, cross = rows_at(pc.block * ROWS, ROWS), rows_at(pc.xblock * ROWS, ROWS)
    ux = lambda t: rcopy(s["u"].at[t, mine, :], s["u"].at[t, mine, :], *sems(2, t), pc.xpeer)
    up = lambda t: rcopy(s["u"].at[t, mine, :], s["u"].at[t, mine, :], *sems(3, t), pc.partner)
    uf = lambda t: rcopy(s["u"].at[t, cross, :], s["u"].at[t, cross, :], *sems(4, t), pc.partner)

    def step(t):
        @pl.when(t < NC)
        def _():
            for i in range(2):
                w_copy(i, t).wait()
                s["p"][t, i] = jnp.dot(hall[...], s["w"][t % WSLOTS, i], preferred_element_type=F32)
            d2d(t).start()

            @pl.when(t + WSLOTS < NC)
            def _():
                for i in range(2):
                    w_copy(i, t + WSLOTS).start()

            wd_copy(t).start()

        @pl.when((t >= 1) & (t < NC + 1))
        def _():
            k = t - 1
            d2d(k).wait_recv()
            o = 1 - pc.x
            for i in range(2):
                s["s1"][k, i] = s["p"][k, i, rows_at(keep + o * ROWS, ROWS), :] + s["r1"][k, i, rows_at(o * ROWS, ROWS), :]
            xco(k).start()

        @pl.when((t >= 3) & (t < NC + 3))
        def _():
            k = t - 3
            xco(k).wait_recv()
            g, u = [
                s["p"][k, i, rows_at(keep + pc.x * ROWS, ROWS), :] + s["r1"][k, i, rows_at(pc.x * ROWS, ROWS), :] + s["r2"][k, i]
                for i in range(2)
            ]
            s["u"][k, mine, :] = (jax.nn.gelu(g, approximate=True) * u).astype(BF16)
            ux(k).start()
            up(k).start()

        @pl.when((t >= 5) & (t < NC + 5))
        def _():
            k = t - 5
            rcopy(s["u"].at[k, cross, :], s["u"].at[k, cross, :], *sems(2, k), pc.xpeer).wait_recv()
            uf(k).start()

        @pl.when(t >= 6)
        def _():
            k = t - 6
            up(k).wait_recv()
            uf(k).wait_recv()
            wd_copy(k).wait()
            acc[...] += lax.dot_general(s["u"][k], s["wd"][k], NT, preferred_element_type=F32)

    acc[...] = jnp.zeros_like(acc)
    loop(NC + 6, step)

    def drain(t):
        for c in (d2d, xco, ux, up, uf):
            c(t).wait_send()

    loop(NC, drain)


def start_ff_weights(s, layer, wg, wu):
    for t in range(WSLOTS):
        for i, ref in enumerate((wg, wu)):
            pltpu.make_async_copy(ref.at[layer, :, pl.ds(t * CH, CH)], s["w"].at[t, i], s["w_sem"].at[t, i]).start()


def gather_heads(pc, s, o_ref):
    mine, cross = rows_at(pc.block * ROWS, ROWS), rows_at(pc.xblock * ROWS, ROWS)
    cs = lambda t: pl.ds(t * OCH, OCH)
    of = s["o"]
    ox, op, fw = [], [], []
    for t in range(NO):
        a = rcopy(o_ref.at[:, cs(t)], of.at[t, mine, :], s["o_s"].at[0, t], s["o_r"].at[0, t], pc.xpeer)
        b = rcopy(o_ref.at[:, cs(t)], of.at[t, mine, :], s["o_s"].at[1, t], s["o_r"].at[1, t], pc.partner)
        a.start()
        b.start()
        ox.append(a)
        op.append(b)
    for t in range(NO):
        of[t, mine, :] = o_ref[:, cs(t)]
    for t in range(NO):
        rcopy(of.at[t, cross, :], of.at[t, cross, :], s["o_s"].at[0, t], s["o_r"].at[0, t], pc.xpeer).wait_recv()
        f = rcopy(of.at[t, cross, :], of.at[t, cross, :], s["o_s"].at[2, t], s["o_r"].at[2, t], pc.partner)
        f.start()
        fw.append(f)
    return ox, op, fw


def qkv_at(w, layer):
    return lambda t: w.at[layer, :, pl.ds(t * QCH, QCH)]


def first_kernel(names, res, gains, wqkv, out, *scratch):
    s = dict(zip(names, scratch))
    pc = Place()
    at = qkv_at(wqkv, 0)
    start_project_weights(s, at)
    barrier_all(pc)
    h = next_norm([res[i] for i in range(4)], gain_rows(gains, 0, 0))
    spread_rows(pc, h, s["h2send"], s["hall2"], s["h2_s"], s["h2_r"])
    project(pc, s, s["hall2"], at, out)


def layer_kernel(names, layer, last, *refs):
    n_in = 7 if last else 8
    res, gains, o_in, wo, wg, wu, wd = refs[:7]
    wqkv = None if last else refs[7]
    res_out = refs[n_in]
    qkv_out = None if last else refs[n_in + 1]
    s = dict(zip(names, refs[n_in + (1 if last else 2):]))
    pc = Place()
    wo_copy = pltpu.make_async_copy(wo.at[layer], s["wo"], s["wo_sem"])
    wo_copy.start()
    start_ff_weights(s, layer, wg, wu)
    barrier_all(pc)
    acc = s["acc"]
    ox, op, fw = gather_heads(pc, s, o_in)
    wo_copy.wait()
    for t in range(NO):
        op[t].wait_recv()
        fw[t].wait_recv()
        total = None
        for j in range(4):
            part = lax.dot_general(s["o"][t, :, j * 256:(j + 1) * 256], s["wo"][t * 4 + j], NT, preferred_element_type=F32)
            total = part if total is None else total + part
        if t == 0:
            acc[...] = total
        else:
            acc[...] += total
    for cp in ox + op + fw:
        cp.wait_send()
    scatter_sums(pc, acc, s["r3"], s["sc_s"], s["sc_r"])
    mids = after_sum([res[i] for i in range(4)], s["r3"], gain_rows(gains, layer, 1))
    for i in range(4):
        s["mid"][i] = mids[i]
    spread_rows(pc, next_norm(mids, gain_rows(gains, layer, 2)), s["hsend"], s["hall"], s["h_s"], s["h_r"])
    if not last:
        at = qkv_at(wqkv, layer + 1)
        start_project_weights(s, at)
    feed_forward(pc, s, layer, s["hall"], wg, wu, wd, s["acc2"])
    scatter_sums(pc, s["acc2"], s["r32"], s["sc2_s"], s["sc2_r"])
    outs = after_sum([s["mid"][i] for i in range(4)], s["r32"], gain_rows(gains, layer, 3))
    if last:
        for i in range(4):
            s["fin"][i] = outs[i]
        peer = pc.other(4)[3]
        cp = rcopy(s["fin"], res_out.at[pc.m], s["fin_s"], s["fin_r"], peer)
        cp.start()
        for i in range(4):
            res_out[pc.m, i] = outs[i]
        cp.wait()
    else:
        for i in range(4):
            res_out[i] = outs[i]
        h = next_norm(outs, gain_rows(gains, layer + 1, 0))
        spread_rows(pc, h, s["h2send"], s["hall2"], s["h2_s"], s["h2_r"])
        project(pc, s, s["hall2"], at, qkv_out)


def q_scratch():
    dma = pltpu.SemaphoreType.DMA
    return {
        "wq": pltpu.VMEM((NQ, WID, QCH), BF16), "wq_sem": dma((NQ,)),
        "qp": pltpu.VMEM((NQ, ALL, QCH), F32), "qr1": pltpu.VMEM((NQ, 64, QCH), F32),
        "qs1": pltpu.VMEM((NQ, ROWS, QCH), F32), "qr2": pltpu.VMEM((NQ, ROWS, QCH), F32),
        "q_s": dma((2, NQ)), "q_r": dma((2, NQ)),
        "h2send": pltpu.VMEM((4, OWN, WID), BF16), "hall2": pltpu.VMEM((ALL, WID), BF16),
        "h2_s": dma((8,)), "h2_r": dma((8,)),
    }


def layer_scratch(last):
    dma = pltpu.SemaphoreType.DMA
    out = {
        "wo": pltpu.VMEM((8, WID, 256), BF16), "wo_sem": dma(()),
        "o": pltpu.VMEM((NO, ALL, OCH), BF16), "o_s": dma((3, NO)), "o_r": dma((3, NO)),
        "acc": pltpu.VMEM((ALL, WID), F32), "acc2": pltpu.VMEM((ALL, WID), F32),
        "r3": pltpu.VMEM((8, OWN, WID), F32), "r32": pltpu.VMEM((8, OWN, WID), F32),
        "sc_s": dma((8,)), "sc_r": dma((8,)), "sc2_s": dma((8,)), "sc2_r": dma((8,)),
        "mid": pltpu.VMEM((4, OWN, WID), BF16),
        "hsend": pltpu.VMEM((4, OWN, WID), BF16), "hall": pltpu.VMEM((ALL, WID), BF16),
        "h_s": dma((8,)), "h_r": dma((8,)),
        "w": pltpu.VMEM((WSLOTS, 2, WID, CH), BF16), "w_sem": dma((WSLOTS, 2)),
        "wd": pltpu.VMEM((NC, WID, CH), BF16), "wd_sem": dma((NC,)),
        "p": pltpu.VMEM((NC, 2, ALL, CH), F32), "r1": pltpu.VMEM((NC, 2, 64, CH), F32),
        "s1": pltpu.VMEM((NC, 2, ROWS, CH), F32), "r2": pltpu.VMEM((NC, 2, ROWS, CH), F32),
        "u": pltpu.VMEM((NC, ALL, CH), BF16),
        "f_s": dma((5, NC)), "f_r": dma((5, NC)),
    }
    if last:
        out.update({"fin": pltpu.VMEM((4, OWN, WID), BF16), "fin_s": dma(()), "fin_r": dma(())})
    else:
        out.update(q_scratch())
    return out


VM = pl.BlockSpec(memory_space=pltpu.VMEM)
HB = pl.BlockSpec(memory_space=pl.ANY)


def params(cid):
    return pltpu.CompilerParams(collective_id=cid, has_side_effects=True, vmem_limit_bytes=67043328)


def call_first(res, gains, wqkv):
    sc = q_scratch()
    return pl.pallas_call(
        functools.partial(first_kernel, tuple(sc)),
        out_shape=jax.ShapeDtypeStruct((ROWS, QW), F32),
        in_specs=[VM, VM, HB], out_specs=VM, scratch_shapes=list(sc.values()),
        compiler_params=params(0), name="qkv0",
    )(res, gains, wqkv)


def call_layer(layer, last, res, gains, o, wo, wg, wu, wd, wqkv):
    sc = layer_scratch(last)
    ins = [res, gains, o, wo, wg, wu, wd] + ([] if last else [wqkv])
    block = jax.ShapeDtypeStruct((2, 4, OWN, WID) if last else (4, OWN, WID), BF16)
    outs = [block] if last else [block, jax.ShapeDtypeStruct((ROWS, QW), F32)]
    return pl.pallas_call(
        functools.partial(layer_kernel, tuple(sc), layer, last),
        out_shape=outs,
        in_specs=[VM, VM, VM] + [HB] * (len(ins) - 3), out_specs=[VM] * len(outs), scratch_shapes=list(sc.values()),
        compiler_params=params(1 + layer), name=f"layer{layer}",
    )(*ins)


def rotary(hidden, cos_t, sin_t):
    half_dim = hidden.shape[-1] // 2
    first_half = hidden[..., :half_dim]
    second_half = hidden[..., half_dim:]
    return jnp.concatenate([first_half * cos_t - second_half * sin_t, second_half * cos_t + first_half * sin_t], axis=-1)


def rope_tables(positions, head_dim):
    inv_freq = ROPE_BASE ** (-jnp.arange(0, head_dim, 2).astype(jnp.float32) / head_dim)
    angles = positions.astype(jnp.float32)[:, None] * inv_freq[None, :]
    return jnp.cos(angles)[:, None, :], jnp.sin(angles)[:, None, :]


def attend(qkv, positions, tables, k_cache, v_cache, is_local):
    n_rows, cache_len, kv_loc, head_dim = k_cache.shape
    cos_t, sin_t = tables
    q_proj = qkv[:, :2048].reshape(n_rows, 8, head_dim)
    k_proj = qkv[:, 2048:3072].reshape(n_rows, 4, head_dim)
    v_new = qkv[:, 3072:].reshape(n_rows, 4, head_dim).astype(BF16)
    q_new = (rotary(q_proj, cos_t, sin_t) * head_dim ** -0.5).astype(BF16)
    k_new = rotary(k_proj, cos_t, sin_t).astype(BF16)
    group_size = q_new.shape[1] // kv_loc
    slot_ids = jnp.arange(cache_len)
    if is_local:
        slot_now = positions % cache_len
        valid_mask = ((positions[:, None] - slot_ids[None, :]) % cache_len) <= positions[:, None]
    else:
        slot_now = positions
        valid_mask = slot_ids[None, :] <= positions[:, None]
    slot_hit = (slot_ids[None, :] == slot_now[:, None])[:, :, None, None]
    k_cache = jnp.where(slot_hit, k_new[:, None], k_cache)
    v_cache = jnp.where(slot_hit, v_new[:, None], v_cache)
    q_grp = q_new.reshape(n_rows, kv_loc, group_size, head_dim)
    scores = jnp.einsum("bkgd,btkd->bkgt", q_grp, k_cache, preferred_element_type=jnp.float32)
    scores = SOFT_CAP * jnp.tanh(scores / SOFT_CAP)
    scores = jnp.where(valid_mask[:, None, None, :], scores, -1e30)
    attn_prob = jax.nn.softmax(scores, axis=-1).astype(jnp.bfloat16)
    head_out = jnp.einsum("bkgt,btkd->bkgd", attn_prob, v_cache, preferred_element_type=jnp.float32)
    return head_out.astype(jnp.bfloat16).reshape(n_rows, 2048), k_cache, v_cache


def solution(mesh):
    def device_step(hidden, positions, k_local, v_local, k_global, v_global, w_q, w_k, w_v, w_o, w_gate, w_up, w_down, norm_gains):
        m = lax.axis_index("model")
        own = lax.dynamic_slice_in_dim(hidden[:, 0, :], m * OWN, OWN, 0)
        res = own.reshape(OWN, 4, WID).transpose(1, 0, 2)
        gains = norm_gains.reshape(2, 4, 4, WID)
        wqkv = jnp.concatenate([w_q.reshape(2, WID, 2048), w_k.reshape(2, WID, 1024), w_v.reshape(2, WID, 1024)], axis=2)
        wo = w_o.transpose(0, 1, 3, 2)
        wd = w_down.transpose(0, 2, 1)
        tables = rope_tables(positions, 256)
        qkv = call_first(res, gains, wqkv)
        heads, k_local, v_local = attend(qkv, positions, tables, k_local, v_local, True)
        res, qkv = call_layer(0, False, res, gains, heads, wo, w_gate, w_up, wd, wqkv)
        heads, k_global, v_global = attend(qkv, positions, tables, k_global, v_global, False)
        out = call_layer(1, True, res, gains, heads, wo, w_gate, w_up, wd, wqkv)
        out = out[0] if isinstance(out, (tuple, list)) else out
        final = out.transpose(0, 2, 1, 3).reshape(ROWS, 1, 4 * WID)
        return final, k_local, v_local, k_global, v_global

    in_specs = (ROW_SPEC, POS_SPEC, CACHE_SPEC, CACHE_SPEC, CACHE_SPEC, CACHE_SPEC, PROJ_IN_SPEC, PROJ_IN_SPEC, PROJ_IN_SPEC, PROJ_OUT_SPEC, FF_IN_SPEC, FF_IN_SPEC, FF_OUT_SPEC, GAIN_SPEC)
    out_specs = (ROW_SPEC, CACHE_SPEC, CACHE_SPEC, CACHE_SPEC, CACHE_SPEC)
    return jax.shard_map(device_step, mesh=mesh, in_specs=in_specs, out_specs=out_specs, check_vma=False)
```

time: 2940 us -> 357 us (0.12)
  waiting for transfers between devices: 2520 us -> 0 us
  Pallas kernels: 0 us -> 236 us
  matrix products: 205 us -> 25 us
  local copies, waits for them, and re-layouts: 146 us -> 54.3 us
    all_gather x14 -> x0, waiting for transfers between devices: 2470 us -> none  [the longest x2 693 us: layer_block(): wd_full = lax.all_gather(w_down[layer], 'data', axis=1, tiled=True)]
    pallas_call x0 -> x3, Pallas kernels: none -> 236 us  [the longest x2 210 us: call_layer(): pl.pallas_call(functools.partial(layer_kernel, tuple(sc), layer, last), o...]
    dot_general x12 -> x0, matrix products: 180 us -> none  [the longest x2 82.5 us: layer_block(): jnp.dot(gated_act, wd_full, preferred_element_type=jnp.float32)]
    slice x7 -> x6, local copies, waits for them, and re-layouts: 79.3 us -> 5.6 us  [the longest x2 1.94 us: attend(): q_proj = qkv[:, :2048].reshape(n_rows, 8, head_dim)]
    psum x4 -> x0, waiting for transfers between devices: 46.7 us -> none  [the longest x2 26.2 us: layer_block(): lax.psum(jnp.dot(gated_act, wd_full, preferred_element_type=jnp.float32),...]
    all_gather x2 -> x0, local copies, waits for them, and re-layouts: 40.6 us -> none  [layer_block(): wo_full = lax.all_gather(w_o[layer], 'data', axis=2, tiled=True)]
    reshape x2 -> x11, local copies, waits for them, and re-layouts: 0.06 us -> 33.6 us  [the longest x1 12.8 us: device_step(): w_q.reshape(2, WID, 2048)]
  transfers between devices with their start and end apart: 18 -> 0, of which waited for: 17 -> 0; matrix products, arithmetic and copies ran while one was open for 9% -> 0% of each run, Pallas kernels for 0% -> 0%
where the time goes in v1:
time: 357 us; the launch traced here: 355 us
  Pallas kernels  236 us (66%)
  local copies, waits for them, and re-layouts  54.3 us (15%)
  other arithmetic  39 us (11%)
  matrix products  25 us (7%)
    pallas_call x2, Pallas kernels, call_layer(): pl.pallas_call(functools.partial(layer_kernel, tuple(sc), layer, last), o...  210 us
    select_n x2, other arithmetic, attend(): k_cache = jnp.where(slot_hit, k_new[:, None], k_cache)  31.1 us
    pallas_call x1, Pallas kernels, call_first(): pl.pallas_call(functools.partial(first_kernel, tuple(sc)), out_shape=jax....  26.1 us
    sub x2, matrix products, attend(): attn_prob = jax.nn.softmax(scores, axis=-1).astype(jnp.bfloat16)  14 us
    reshape x1, local copies, waits for them, and re-layouts, device_step(): w_q.reshape(2, WID, 2048)  12.8 us
    dot_general x2, matrix products, attend(): jnp.einsum('bkgt,btkd->bkgd', attn_prob, v_cache, preferred_element_type=...  11 us
    unnamed x12, local copies, waits for them, and re-layouts  10.6 us
    reshape x1, local copies, waits for them, and re-layouts, device_step(): w_k.reshape(2, WID, 1024)  7.83 us

profile of v1, /device:TPU:0, one launch (start us, length us, event | category | flops | bytes accessed | tf_op | source)
XLA Modules:
  0.0 355.2 jit_solution(13955395237834370609)
XLA Ops:
  0.6 0.7 fusion.62
  1.4 0.7 iota_compare_fusion.2
  2.1 1.3 fusion.53
  3.4 1.3 iota_compare_fusion.1
  4.7 0.8 multiply_cosine_fusion
  5.5 1.6 reshape.249.gains.refs_1_
  7.1 0.9 constant_dynamic-slice_fusion
  8.0 0.2 reshape.248
  8.2 0.7 copy.64
  8.9 7.8 %reshape.251 = bf16[2,960,1024]{2,1,0:T(8,128)(2,1)} reshape(bf16[2,960,4,256]{3,2,1,0:T(4,128)(2,1)} %param.21) | data formatting | bytes 7864320 | tf_op jit(solution)/shard_map/reshape | solution.py:458
  16.7 7.8 %reshape.252 = bf16[2,960,1024]{2,1,0:T(8,128)(2,1)} reshape(bf16[2,960,4,256]{3,2,1,0:T(4,128)(2,1)} %param.22) | data formatting | bytes 7864320 | tf_op jit(solution)/shard_map/reshape | solution.py:458
  24.5 12.8 %reshape.250 = bf16[2,960,2048]{2,1,0:T(8,128)(2,1)} reshape(bf16[2,960,8,256]{3,2,1,0:T(8,128)(2,1)} %param.20) | data formatting | bytes 15728640 | tf_op jit(solution)/shard_map/reshape | solution.py:458
  37.4 0.0 copy-start.1
  37.4 0.0 copy-start
  37.4 8.1 %constant_dynamic-update-slice_fusion.2 = bf16[2,960,4096]{2,1,0:T(8,128)(2,1)} fusion(bf16[2,960,2048]{2,1,0:T(8,128)(2,1)} %reshape.250), kind=kLoop, calls=%fused_computation.66 | loop fusion | bytes 15728640
  45.5 0.0 copy-done.1
  45.5 2.3 constant_dynamic-update-slice_fusion.1
  47.8 0.0 copy-done
  47.8 2.3 constant_dynamic-update-slice_fusion.wqkv.refs_7_
  50.2 26.1 %qkv0.1 = f32[32,4096]{1,0:T(8,128)} custom-call(bf16[4,16,960]{2,1,0:T(8,128)(2,1)} %bitcast.22, bf16[2,4,4,960]{3,2,1,0:T(4,128)(2,1)} %reshape.249.gains.refs_1_, bf16[2,960,4096]{2,1,0:T(8,128)(2,1)} %constant_dynamic-update-slice_fusion.wqkv.refs_7_), custom_call_target="tpu_custom_call" | custom-call | tf_op jit(solution)/shard_map/qkv0/pallas_call | solution.py:390
  76.2 0.0 copy-start.3
  76.3 0.9 slice.87
  77.2 0.9 slice.47
  78.1 1.0 slice.44
  79.1 0.1 copy.29
  79.2 0.1 reshape.254
  79.3 0.8 subtract_convert_fusion.1
  80.1 0.8 multiply_subtract_fusion.1
  80.8 8.3 %broadcast_select_fusion.3 = (bf16[32,64,4,256]{3,2,1,0:T(4,128)(2,1)}, bf16[32,64,4,256]{3,2,1,0:T(4,128)(2,1)}) fusion(bf16[32,64,4,256]{3,2,1,0:T(4,128)(2,1)} %param.16, pred[32,64]{1,0:T(8,128)(4,1)} %iota_compare_fusion.2, bf16[32,4,256]{2,1,0:T(4,128)(2,1)S(1)} %pad_maximum_fusion, bf16[32,64,4,256]{3,2,1,0:T(4,128)(2,1)} %param.17, ...), kind=kLoop, calls=%fused_computation.13 | loop fusion | flops 4194304 | bytes 16910336 | tf_op jit(solution)/shard_map/jit(_where)/select_n | solution.py:441
  89.2 0.0 copy-done.3
  89.2 3.6 %fusion.63 = (f32[32,4,2]{2,1,0:T(4,128)S(1)}, f32[32,4,2,64]{3,2,1,0:T(2,128)S(1)}) fusion(bf16[32,64,4,256]{3,2,1,0:T(4,128)(2,1)} %get-tuple-element.19, f32[32,4,2,128]{3,2,1,0:T(2,128)S(1)} %bitcast.32, f32[32,4,2,128]{3,2,1,0:T(2,128)S(1)} %bitcast.31, pred[32,64]{1,0:T(8,128)(4,1)S(1)} %copy-done.3), kind=kOutput, calls=%fused_computation.78 | convolution fusion | flops 8667199 | bytes 4525056 | tf_op jit(solution)/shard_map/sub | solution.py:447
  92.7 2.9 fusion.13
  95.7 0.7 reshape.255.refs_2_
  96.4 113.1 %layer0.1 = (bf16[4,16,960]{2,1,0:T(8,128)(2,1)}, f32[32,4096]{1,0:T(8,128)}) custom-call(bf16[4,16,960]{2,1,0:T(8,128)(2,1)} %bitcast.23, bf16[2,4,4,960]{3,2,1,0:T(4,128)(2,1)} %reshape.249.gains.refs_1_, bf16[32,2048]{1,0:T(8,128)(2,1)} %reshape.255.refs_2_, bf16[2,8,960,256]{3,2,1,0:T(8,128)(2,1)} %bitcast.20, bf16[2,960,7680]{2,1,0:T(8,128)(2,1)} %refs_4_.3, ...), custom_call_target="tpu_custom_call" | custom-call | tf_op jit(solution)/shard_map/layer0/pallas_call | solution.py:403
  209.5 0.9 slice.86
  210.5 0.9 slice.54
  211.4 1.0 slice.51
  212.4 0.1 copy.30
  212.5 0.1 reshape.257
  212.6 0.8 subtract_convert_fusion
  213.3 0.8 multiply_subtract_fusion
  214.1 0.0 copy-start.2
  214.2 22.7 %broadcast_select_fusion.1 = (bf16[32,256,4,256]{3,2,1,0:T(4,128)(2,1)}, bf16[32,256,4,256]{3,2,1,0:T(4,128)(2,1)}) fusion(bf16[32,256,4,256]{3,2,1,0:T(4,128)(2,1)} %param.18, pred[32,256]{1,0:T(8,128)(4,1)} %get-tuple-element.24, bf16[32,4,256]{2,1,0:T(4,128)(2,1)S(1)} %pad_maximum_fusion.1, bf16[32,256,4,256]{3,2,1,0:T(4,128)(2,1)} %param.19, ...), kind=kLoop, calls=%fused_computation.7 | loop fusion | flops 16777216 | bytes 67248128 | tf_op jit(solution)/shard_map/jit(_where)/select_n | solution.py:441
  236.9 0.0 copy-done.2
  236.9 10.4 %fusion.64 = (f32[32,4,2]{2,1,0:T(4,128)S(1)}, f32[32,4,2,256]{3,2,1,0:T(2,128)S(1)}) fusion(bf16[32,256,4,256]{3,2,1,0:T(4,128)(2,1)} %get-tuple-element.17, pred[32,256]{1,0:T(8,128)(4,1)S(1)} %copy-done.2, f32[32,4,2,128]{3,2,1,0:T(2,128)S(1)} %bitcast.30, f32[32,4,2,128]{3,2,1,0:T(2,128)S(1)} %bitcast.29), kind=kOutput, calls=%fused_computation.79 | convolution fusion | flops 34078976 | bytes 17310720 | tf_op jit(solution)/shard_map/sub | solution.py:447
  247.3 8.1 %fusion.16 = bf16[32,4,2,256]{3,2,1,0:T(2,128)(2,1)S(1)} fusion(bf16[32,256,4,256]{3,2,1,0:T(4,128)(2,1)} %get-tuple-element.18, f32[32,4,2,256]{3,2,1,0:T(2,128)S(1)} %get-tuple-element.30, f32[32,4,2]{2,1,0:T(4,128)S(1)} %get-tuple-element.29), kind=kOutput, calls=%fused_computation.18 | convolution fusion | flops 33751040 | bytes 17171456 | tf_op jit(solution)/shard_map/bkgt,btkd->bkgd/dot_general | solution.py:448
  255.4 0.7 reshape.258.refs_2_
  256.1 96.9 %layer1.1 = bf16[2,4,16,960]{3,2,1,0:T(8,128)(2,1)} custom-call(bf16[4,16,960]{2,1,0:T(8,128)(2,1)} %get-tuple-element.7.refs_0_, bf16[2,4,4,960]{3,2,1,0:T(4,128)(2,1)} %reshape.249.gains.refs_1_, bf16[32,2048]{1,0:T(8,128)(2,1)} %reshape.258.refs_2_, bf16[2,8,960,256]{3,2,1,0:T(8,128)(2,1)} %bitcast.21, bf16[2,960,7680]{2,1,0:T(8,128)(2,1)} %refs_4_.3, ...), custom_call_target="tpu_custom_call" | custom-call | tf_op jit(solution)/shard_map/layer1/pallas_call | solution.py:403
  353.0 1.2 copy.28
  354.2 1.0 reshape.259
  (5 shorter events, 0.1 us)
Async XLA Ops:
  37.4 8.1 %copy-start.1 = (bf16[2,960,1024]{2,1,0:T(8,128)(2,1)S(1)}, bf16[2,960,1024]{2,1,0:T(8,128)(2,1)}, u32[]{:S(2)}) copy-start(bf16[2,960,1024]{2,1,0:T(8,128)(2,1)} %reshape.251) | copy-start | bytes 11796484
  37.4 10.5 %copy-start = (bf16[2,960,1024]{2,1,0:T(8,128)(2,1)S(1)}, bf16[2,960,1024]{2,1,0:T(8,128)(2,1)}, u32[]{:S(2)}) copy-start(bf16[2,960,1024]{2,1,0:T(8,128)(2,1)} %reshape.252) | copy-start | bytes 11796484
  76.2 12.9 %copy-start.3 = (pred[32,64]{1,0:T(8,128)(4,1)S(1)}, pred[32,64]{1,0:T(8,128)(4,1)}, u32[]{:S(2)}) copy-start(pred[32,64]{1,0:T(8,128)(4,1)} %fusion.53) | copy-start | bytes 6148
  214.1 22.8 %copy-start.2 = (pred[32,256]{1,0:T(8,128)(4,1)S(1)}, pred[32,256]{1,0:T(8,128)(4,1)}, u32[]{:S(2)}) copy-start(pred[32,256]{1,0:T(8,128)(4,1)} %get-tuple-element.23) | copy-start | bytes 24580
